TPU v7x, 32 devices: a whole 2x2x4 slice. The times are simulated.
32 devices in a mesh: groups: 2 (over y), gx: 4 (over z), gy: 4 (over x, core).
Axes of the slice: x: 2, y: 2, z: 4, core: 2. Of those that a mesh axis runs over, the one named last changes fastest.
Arguments:
- thermal_deviation: float32 [32, 256, 512], P('groups', 'gy', 'gx'), parts along dimension 0, may hold values from -6 to 6
- brine_content: float32 [32, 256, 512], P('groups', 'gy', 'gx'), parts along dimension 0, may hold values from 0.2 to 2.4
- current_components: float32 [4, 16, 256, 512], P('groups', None, 'gy', 'gx'), parts along dimension 0, may hold values from -4 to 4
- sea_indicator: int32 [256, 512], P('gy', 'gx'), may hold values from 0 to 1, as said below
- flooded_layer_number: int32 [256, 512], P('gy', 'gx'), may hold values from 1 to 16
- footprint_square_metres: float32 [256, 512], P('gy', 'gx'), may hold values from 0.5 to 5
- rainfall_input: float32 [256, 512], P('gy', 'gx'), may hold values from -2 to 3.5
- seam_partner_index: int32 [512], P('gx'), may hold values from 0 to 511, as said below
Outputs:
- temperature_next: float32 [32, 256, 512], P('groups', 'gy', 'gx'), parts along dimension 0
- salinity_next: float32 [32, 256, 512], P('groups', 'gy', 'gx'), parts along dimension 0
There are 2 independent parts, one for each index of `groups`. A program takes and returns all parts, laid end to end along the dimension named above; an argument that names none is the same for every part. Nothing has to cross between parts.
Inputs may be any that keep to these rules, and one draw needn't show every extreme that they name: `sea_indicator`: at least one column is ocean. seam_partner_index[x] = (s - x) mod 512 for one s of each draw with s mod 128 = 127; the map is its own inverse and has no fixed point.
All inputs are finite; a program needn't handle non-finite values.
Results may differ from a plain program's by a relative error of at most 0.00002.
Values sent between devices are 32-bit elements; how exact they have to be, the bound alone decides.
A program may use at most 64 MiB of HBM per device.

v0:
```python
import functools

import jax
import jax.numpy as jnp
from jax import lax
from jax.experimental import pallas as pl
from jax.experimental.pallas import tpu as pltpu
from jax.sharding import PartitionSpec as P

time_step = 0.25
diffusivity = 0.5
vertical_mixing = 0.3
top_thickness = 0.5

MESH = pl.DeviceIdType.MESH


def repeat(count, body):
    if count <= 16:
        for i in range(count):
            body(i)
    else:
        pl.loop(0, count)(body)


def face_weights(speed, open_face):
    near_weight = jnp.where(open_face, jnp.maximum(speed, 0.0) + diffusivity, 0.0)
    far_weight = jnp.where(open_face, jnp.minimum(speed, 0.0) - diffusivity, 0.0)
    return near_weight, far_weight


def kernel(
    nx, ny, nk, h, w,
    t_hbm, s_hbm, uv_hbm, sea_hbm, lay_hbm, area_hbm, rain_hbm, seam_hbm,
    t_out, s_out,
    t_v, s_v, uv_v, sea_v, lay_v, area_v, rain_v, s0_v, g_v, depth_v,
    pack_v, last_v, first_v, east_v, west_v, up_v, down_v, south_v, north_v, fold_v,
    part_v, parts_v, seam_smem,
    load_sems, pack_send, pack_recv, row_send, row_recv, fold_send, fold_recv,
    part_send, part_recv,
):
    mx, my = lax.axis_index("gx"), lax.axis_index("gy")
    is_top = my == ny - 1
    peers = nx * ny - 1

    def peer(r):
        r = r + 1
        return {"gx": lax.rem(mx + r // ny, nx), "gy": lax.rem(my + r % ny, ny)}

    barrier = pltpu.get_barrier_semaphore()

    def greet(r):
        pl.semaphore_signal(barrier, inc=1, device_id=peer(r), device_id_type=MESH)

    loads = [
        pltpu.make_async_copy(src, dst, load_sems.at[i])
        for i, (src, dst) in enumerate(
            [
                (area_hbm, area_v),
                (sea_hbm, sea_v),
                (rain_hbm, rain_v),
                (s_hbm.at[pl.ds(0, h)], s0_v),
                (lay_hbm, lay_v),
                (t_hbm, t_v),
                (s_hbm, s_v),
                (uv_hbm.at[pl.ds(0, nk * h)], uv_v.at[pl.ds(0, nk * h)]),
                (uv_hbm.at[pl.ds(nk * h, nk * h)], uv_v.at[pl.ds(nk * h, nk * h)]),
                (seam_hbm, seam_smem),
            ]
        )
    ]
    for load in loads[:4]:
        load.start()
    repeat(peers, greet)
    for load in loads[4:]:
        load.start()

    for load in loads[:4]:
        load.wait()
    area = area_v[...]
    sea = sea_v[...]
    wet_area = area * sea.astype(jnp.float32)
    surface = s0_v[...]
    fresh = wet_area * rain_v[...]
    row8 = lax.broadcasted_iota(jnp.int32, (8, w), 0)
    part = jnp.zeros((8, w), jnp.float32)
    for i, term in enumerate((wet_area, fresh, fresh * surface, wet_area * surface)):
        part = jnp.where(row8 == i, jnp.sum(term, axis=0, keepdims=True), part)
    part_v[...] = part
    gain = time_step / area
    g_v[...] = gain

    pl.semaphore_wait(barrier, peers)

    def part_copy(r):
        return pltpu.make_async_remote_copy(
            src_ref=part_v, dst_ref=parts_v.at[r],
            send_sem=part_send.at[r], recv_sem=part_recv.at[r],
            device_id=peer(r), device_id_type=MESH,
        )

    repeat(peers, lambda r: part_copy(r).start())

    for load in loads[4:]:
        load.wait()
    depth = (sea * lay_v[...]).astype(jnp.float32)
    depth_v[...] = depth

    lane = lax.broadcasted_iota(jnp.int32, (h, w), 1)
    pair = lane // 2
    packed = jnp.zeros((h, w), jnp.float32)
    for i, ref in enumerate((t_v, s_v, uv_v)):
        for k in range(nk):
            j = i * nk + k
            packed = jnp.where(pair == j, pltpu.roll(ref[pl.ds(k * h, h), :], 2 * j + 1, 1), packed)
    depth_at = 6 * nk
    packed = jnp.where(pair == 3 * nk, pltpu.roll(depth, depth_at + 1, 1), packed)
    pack_v[...] = packed
    half = h // 2
    even_half = lane[:half] % 2 == 0
    last_v[...] = jnp.where(even_half, packed[:half], pltpu.roll(packed[half:], 1, 1))
    first_v[...] = jnp.where(even_half, pltpu.roll(packed[half:], w - 1, 1), packed[:half])

    to_east = pltpu.make_async_remote_copy(
        src_ref=last_v, dst_ref=west_v, send_sem=pack_send.at[0], recv_sem=pack_recv.at[0],
        device_id={"gx": lax.rem(mx + 1, nx)}, device_id_type=MESH,
    )
    to_west = pltpu.make_async_remote_copy(
        src_ref=first_v, dst_ref=east_v, send_sem=pack_send.at[1], recv_sem=pack_recv.at[1],
        device_id={"gx": lax.rem(mx + nx - 1, nx)}, device_id_type=MESH,
    )
    to_east.start()
    to_west.start()

    def rows(ref, row, base=0):
        return ref[pl.ds(base + row, nk, stride=h), :]

    up_v[pl.ds(0, nk), :] = rows(t_v, h - 1)
    up_v[pl.ds(nk, nk), :] = rows(s_v, h - 1)
    up_v[pl.ds(2 * nk, nk), :] = rows(uv_v, h - 1, nk * h)
    up_v[pl.ds(3 * nk, 8), :] = jnp.broadcast_to(depth[h - 1 : h, :], (8, w))
    down_v[pl.ds(0, nk), :] = rows(t_v, 0)
    down_v[pl.ds(nk, nk), :] = rows(s_v, 0)
    down_v[pl.ds(2 * nk, 8), :] = jnp.broadcast_to(depth[0:1, :], (8, w))

    @pl.when(is_top)
    def _():
        up = up_v[...]
        flip = (w - 1) - lax.broadcasted_iota(jnp.int32, up.shape, 1)
        fold_v[mx] = jnp.take_along_axis(up, flip, axis=1)

    to_north = pltpu.make_async_remote_copy(
        src_ref=up_v, dst_ref=south_v, send_sem=row_send.at[0], recv_sem=row_recv.at[0],
        device_id={"gy": lax.rem(my + 1, ny)}, device_id_type=MESH,
    )
    to_south = pltpu.make_async_remote_copy(
        src_ref=down_v, dst_ref=north_v, send_sem=row_send.at[1], recv_sem=row_recv.at[1],
        device_id={"gy": lax.rem(my + ny - 1, ny)}, device_id_type=MESH,
    )

    def fold_copy(d):
        return pltpu.make_async_remote_copy(
            src_ref=fold_v.at[mx], dst_ref=fold_v.at[mx],
            send_sem=fold_send.at[d], recv_sem=fold_recv.at[d],
            device_id={"gx": lax.rem(mx + d + 1, nx)}, device_id_type=MESH,
        )


    @pl.when(jnp.logical_not(is_top))
    def _():
        to_north.start()

    @pl.when(my > 0)
    def _():
        to_south.start()

    @pl.when(is_top)
    def _():
        repeat(nx - 1, lambda d: fold_copy(d).start())

    row = lax.broadcasted_iota(jnp.int32, (h, w), 0)
    depth_east = jnp.where(lane == w - 1, 0.0, jnp.minimum(depth, pltpu.roll(depth, w - 1, 1)))
    depth_north = jnp.where(row == h - 1, 0.0, jnp.minimum(depth, pltpu.roll(depth, h - 1, 0)))

    def level(k, above):
        kf = k.astype(jnp.float32)
        at = pl.ds(pl.multiple_of(k * h, h), h)
        below = pl.ds(pl.multiple_of(jnp.minimum(k + 1, nk - 1) * h, h), h)
        east_near, east_far = face_weights(uv_v[at, :], depth_east > kf)
        north_near, north_far = face_weights(
            uv_v[pl.ds(pl.multiple_of((k + nk) * h, h), h), :], depth_north > kf
        )
        mix = jnp.where(depth_v[...] > kf + 1.0, time_step * vertical_mixing, 0.0)
        gain = g_v[...]
        falls = []
        for ref, out, came in ((t_v, t_out, above[0]), (s_v, s_out, above[1])):
            c = ref[at, :]
            east = east_near * c + east_far * pltpu.roll(c, w - 1, 1)
            north = north_near * c + north_far * pltpu.roll(c, h - 1, 0)
            flow = (pltpu.roll(east, 1, 1) - east) + (pltpu.roll(north, 1, 0) - north)
            fall = mix * (c - ref[below, :])
            out[at, :] = c + (gain * flow + (came - fall))
            falls.append(fall)
        return tuple(falls)

    zero = jnp.zeros((h, w), jnp.float32)
    lax.fori_loop(0, nk, level, (zero, zero))

    level_row = lax.broadcasted_iota(jnp.int32, (nk, w), 0).astype(jnp.float32)

    def north_edge(far_t, far_s, speed, far_depth):
        near_weight, far_weight = face_weights(
            speed, jnp.minimum(up_v[3 * nk : 3 * nk + 1, :], far_depth) > level_row
        )
        for near, far, out in (
            (up_v[pl.ds(0, nk), :], far_t, t_out),
            (up_v[pl.ds(nk, nk), :], far_s, s_out),
        ):
            at = pl.ds(h - 1, nk, stride=h)
            out[at, :] -= g_v[h - 1 : h, :] * (near_weight * near + far_weight * far)

    @pl.when(jnp.logical_not(is_top))
    def _():
        to_north.wait_send()
        to_south.wait_recv()
        north_edge(
            north_v[pl.ds(0, nk), :],
            north_v[pl.ds(nk, nk), :],
            up_v[pl.ds(2 * nk, nk), :],
            north_v[2 * nk : 2 * nk + 1, :],
        )

    @pl.when(my > 0)
    def _():
        to_south.wait_send()
        to_north.wait_recv()
        near_weight, far_weight = face_weights(
            south_v[pl.ds(2 * nk, nk), :],
            jnp.minimum(down_v[2 * nk : 2 * nk + 1, :], south_v[3 * nk : 3 * nk + 1, :]) > level_row,
        )
        for i, out in enumerate((t_out, s_out)):
            at = pl.ds(0, nk, stride=h)
            out[at, :] += g_v[0:1, :] * (
                near_weight * south_v[pl.ds(i * nk, nk), :]
                + far_weight * down_v[pl.ds(i * nk, nk), :]
            )

    to_east.wait()
    to_west.wait()
    mine, east_half, west_half = pack_v[...], east_v[...], west_v[...]
    east_side = jnp.concatenate([east_half, pltpu.roll(east_half, 1, 1)], axis=0)
    west_side = jnp.concatenate([west_half, pltpu.roll(west_half, w - 1, 1)], axis=0)
    even = lane % 2 == 0

    def speeds(cells):
        return jnp.where(
            pair < nk, pltpu.roll(cells, w - 4 * nk, 1), pltpu.roll(cells, w - 2 * nk, 1)
        )

    def column(cells, at):
        return jnp.broadcast_to(cells[:, at : at + 1], (h, w))

    near = jnp.where(even, mine, pltpu.roll(west_side, 1, 1))
    far = jnp.where(even, pltpu.roll(east_side, w - 1, 1), mine)
    speed = jnp.where(even, speeds(mine), pltpu.roll(speeds(west_side), 1, 1))
    shallow = jnp.where(
        even,
        jnp.minimum(column(mine, depth_at), column(east_side, depth_at + 1)),
        jnp.minimum(column(mine, depth_at + 1), column(west_side, depth_at)),
    )
    near_weight, far_weight = face_weights(speed, shallow > (pair % nk).astype(jnp.float32))
    gain = g_v[...]
    edge_gain = jnp.where(even, -column(gain, w - 1), column(gain, 0))
    edge = edge_gain * (near_weight * near + far_weight * far)
    at_edge = (lane == 0) | (lane == w - 1)
    for i, out in enumerate((t_out, s_out)):
        for k in range(nk):
            shift = (w - (2 * (i * nk + k) + 1)) % w
            out[pl.ds(k * h, h), :] += jnp.where(at_edge, pltpu.roll(edge, shift, 1), 0.0)

    @pl.when(is_top)
    def _():
        repeat(nx - 1, lambda d: fold_copy(d).wait())
        partner = fold_v[seam_smem[0] // w]
        north_edge(
            partner[:nk],
            partner[nk : 2 * nk],
            0.5 * (up_v[pl.ds(2 * nk, nk), :] - partner[2 * nk : 3 * nk]),
            partner[3 * nk : 3 * nk + 1],
        )

    repeat(peers, lambda r: part_copy(r).wait())
    totals = part_v[...] + jnp.sum(parts_v[...], axis=0)
    totals = jnp.sum(totals, axis=1, keepdims=True)
    total_area, total_fresh = totals[0:1], totals[1:2]
    salt_fresh, salt_only = totals[2:3], totals[3:4]
    mean_fresh = total_fresh / total_area
    lift = (salt_fresh - mean_fresh * salt_only) / total_area
    virtual = lift - s0_v[...] * (rain_v[...] - mean_fresh)
    s_out[pl.ds(0, h), :] += jnp.where(depth_v[...] > 0.0, time_step / top_thickness * virtual, 0.0)


store_cuts = 1


def store_kernel(t_ref, s_ref, t_out, s_out, sems):
    step = t_ref.shape[0] // store_cuts
    copies = [
        pltpu.make_async_copy(
            src.at[pl.ds(i * step, step)], dst.at[pl.ds(i * step, step)], sems.at[2 * i + n]
        )
        for i in range(store_cuts)
        for n, (src, dst) in enumerate(((t_ref, t_out), (s_ref, s_out)))
    ]
    for copy in copies:
        copy.start()
    for copy in copies:
        copy.wait()


def shards(nx, ny, t, s, uv, sea, layers, area, rain, seam):
    nk, h, w = t.shape
    assert w == 128 and h % 16 == 0 and nk % 8 == 0 and 6 * nk + 2 <= w
    f32 = jnp.float32
    peers = nx * ny - 1
    half_plane = pltpu.VMEM((h // 2, w), f32)
    any_space = pl.BlockSpec(memory_space=pl.ANY)
    dma = pltpu.SemaphoreType.DMA
    plane = pltpu.VMEM((h, w), f32)
    t_next, s_next = pl.pallas_call(
        functools.partial(kernel, nx, ny, nk, h, w),
        out_shape=[pltpu.VMEM((nk * h, w), f32)] * 2,
        in_specs=[any_space] * 8,
        out_specs=[pl.BlockSpec(memory_space=pltpu.VMEM)] * 2,
        scratch_shapes=[
            pltpu.VMEM((nk * h, w), f32),
            pltpu.VMEM((nk * h, w), f32),
            pltpu.VMEM((2 * nk * h, w), f32),
            pltpu.VMEM((h, w), jnp.int32),
            pltpu.VMEM((h, w), jnp.int32),
            plane, plane, plane, plane, plane,
            plane, half_plane, half_plane, half_plane, half_plane,
            pltpu.VMEM((3 * nk + 8, w), f32),
            pltpu.VMEM((2 * nk + 8, w), f32),
            pltpu.VMEM((3 * nk + 8, w), f32),
            pltpu.VMEM((2 * nk + 8, w), f32),
            pltpu.VMEM((nx, 3 * nk + 8, w), f32),
            pltpu.VMEM((8, w), f32),
            pltpu.VMEM((peers, 8, w), f32),
            pltpu.SMEM((w,), jnp.int32),
            dma((10,)), dma((2,)), dma((2,)), dma((2,)), dma((2,)),
            dma((nx - 1,)), dma((nx - 1,)), dma((peers,)), dma((peers,)),
        ],
        compiler_params=pltpu.CompilerParams(
            collective_id=0, has_side_effects=True, vmem_limit_bytes=65990000
        ),
        name="tracer_step",
    )(
        t.reshape(nk * h, w), s.reshape(nk * h, w), uv.reshape(2 * nk * h, w),
        sea, layers, area, rain, seam,
    )
    t_next, s_next = pl.pallas_call(
        store_kernel,
        out_shape=[jax.ShapeDtypeStruct((nk * h, w), f32)] * 2,
        in_specs=[any_space] * 2,
        out_specs=[any_space] * 2,
        scratch_shapes=[dma((2 * store_cuts,))],
        compiler_params=pltpu.CompilerParams(vmem_limit_bytes=8 << 20),
        name="store",
    )(t_next, s_next)
    return t_next.reshape(t.shape), s_next.reshape(s.shape)


def solution(mesh):
    in_specs = (
        P("groups", "gy", "gx"),
        P("groups", "gy", "gx"),
        P("groups", None, "gy", "gx"),
        P("gy", "gx"),
        P("gy", "gx"),
        P("gy", "gx"),
        P("gy", "gx"),
        P("gx"),
    )
    out_specs = (P("groups", "gy", "gx"), P("groups", "gy", "gx"))
    return jax.shard_map(
        functools.partial(shards, mesh.shape["gx"], mesh.shape["gy"]),
        mesh=mesh, in_specs=in_specs, out_specs=out_specs, check_vma=False,
    )
```

profile of v0, /device:TPU:0, one launch (start us, length us, event | category | flops | bytes accessed | tf_op | source)
XLA Modules:
  0.0 12.2 jit_solution(6812490673957184612)
XLA Ops:
  0.6 10.6 %tracer_step.1 = (f32[1024,128]{1,0:T(8,128)S(1)}, f32[1024,128]{1,0:T(8,128)S(1)}) custom-call(f32[1024,128]{1,0:T(8,128)} %bitcast.6, f32[1024,128]{1,0:T(8,128)} %bitcast.7, f32[2048,128]{1,0:T(8,128)} %bitcast.5, s32[64,128]{1,0:T(8,128)} %sea_hbm.1, s32[64,128]{1,0:T(8,128)} %lay_hbm.1, f32[64,128]{1,0:T(8,128)} %area_hbm.1, f32[64,128]{1,0:T(8,128)} %rain_hbm.1, ...), custom_call_target="tpu_custom_call" | custom-call | tf_op jit(solution)/shard_map/tracer_step/pallas_call | solution.py:330
  11.3 1.0 %store.1 = (f32[1024,128]{1,0:T(8,128)}, f32[1024,128]{1,0:T(8,128)}) custom-call(f32[1024,128]{1,0:T(8,128)S(1)} %get-tuple-element.6.t_ref, f32[1024,128]{1,0:T(8,128)S(1)} %get-tuple-element.7.s_ref), custom_call_target="tpu_custom_call" | custom-call | tf_op jit(solution)/shard_map/store/pallas_call | solution.py:362
where the time goes:
time: 12.4 us; the launch traced here: 12.2 us
  Pallas kernels  11.6 us (94%)
  between operations  0.64 us (5%)
    pallas_call x1, Pallas kernels, shards(): pl.pallas_call(functools.partial(kernel, nx, ny, nk, h, w), out_shape=[pl...  10.6 us
    pallas_call x1, Pallas kernels, shards(): pl.pallas_call(store_kernel, out_shape=[jax.ShapeDtypeStruct((nk * h, w),...  0.99 us

commit v1 on v0

v1 whole, which is shorter than its diff:
```python
import functools

import jax
import jax.numpy as jnp
from jax import lax
from jax.experimental import pallas as pl
from jax.experimental.pallas import tpu as pltpu
from jax.sharding import PartitionSpec as P

time_step = 0.25
diffusivity = 0.5
vertical_mixing = 0.3
top_thickness = 0.5

MESH = pl.DeviceIdType.MESH


def repeat(count, body):
    if count <= 16:
        for i in range(count):
            body(i)
    else:
        pl.loop(0, count)(body)


def face_weights(speed, open_face):
    near_weight = jnp.where(open_face, jnp.maximum(speed, 0.0) + diffusivity, 0.0)
    far_weight = jnp.where(open_face, jnp.minimum(speed, 0.0) - diffusivity, 0.0)
    return near_weight, far_weight


def kernel(
    nx, ny, nk, h, w,
    t_hbm, s_hbm, uv_hbm, sea_hbm, lay_hbm, area_hbm, rain_hbm, seam_hbm,
    t_out, s_out, edge_out,
    t_v, s_v, uv_v, sea_v, lay_v, area_v, rain_v, s0_v, g_v, depth_v,
    pack_v, last_v, first_v, east_v, west_v, up_v, down_v, south_v, north_v, fold_v,
    part_v, parts_v, seam_smem,
    load_sems, pack_send, pack_recv, row_send, row_recv, fold_send, fold_recv,
    part_send, part_recv,
):
    mx, my = lax.axis_index("gx"), lax.axis_index("gy")
    is_top = my == ny - 1
    peers = nx * ny - 1

    def peer(r):
        r = r + 1
        return {"gx": lax.rem(mx + r // ny, nx), "gy": lax.rem(my + r % ny, ny)}

    barrier = pltpu.get_barrier_semaphore()

    def greet(r):
        pl.semaphore_signal(barrier, inc=1, device_id=peer(r), device_id_type=MESH)

    loads = [
        pltpu.make_async_copy(src, dst, load_sems.at[i])
        for i, (src, dst) in enumerate(
            [
                (area_hbm, area_v),
                (sea_hbm, sea_v),
                (rain_hbm, rain_v),
                (s_hbm.at[pl.ds(0, h)], s0_v),
                (lay_hbm, lay_v),
                (t_hbm, t_v),
                (s_hbm, s_v),
                (uv_hbm.at[pl.ds(0, nk * h)], uv_v.at[pl.ds(0, nk * h)]),
                (uv_hbm.at[pl.ds(nk * h, nk * h)], uv_v.at[pl.ds(nk * h, nk * h)]),
                (seam_hbm, seam_smem),
            ]
        )
    ]
    for load in loads[:4]:
        load.start()
    repeat(peers, greet)
    for load in loads[4:]:
        load.start()

    for load in loads[:4]:
        load.wait()
    area = area_v[...]
    sea = sea_v[...]
    wet_area = area * sea.astype(jnp.float32)
    surface = s0_v[...]
    fresh = wet_area * rain_v[...]
    lane1 = lax.broadcasted_iota(jnp.int32, (1, w), 1)
    part = jnp.zeros((1, w), jnp.float32)
    for i, term in enumerate((wet_area, fresh, fresh * surface, wet_area * surface)):
        rows8 = jnp.sum(term.reshape(h // 8, 8, w), axis=0)
        part = jnp.where(
            lane1 == i, jnp.sum(jnp.sum(rows8, axis=1, keepdims=True), axis=0, keepdims=True), part
        )
    part_v[...] = part
    gain = time_step / area
    g_v[...] = gain

    me = mx * ny + my
    parts_v[me] = part

    def send_part(r):
        @pl.when(r != me)
        def _():
            pltpu.make_async_remote_copy(
                src_ref=part_v, dst_ref=parts_v.at[me], send_sem=part_send, recv_sem=part_recv,
                device_id={"gx": r // ny, "gy": r % ny}, device_id_type=MESH,
            ).start()

    others = parts_v.at[pl.ds(0, peers)]
    all_parts = pltpu.make_async_remote_copy(
        src_ref=others, dst_ref=others, send_sem=part_send, recv_sem=part_recv,
        device_id=peer(0), device_id_type=MESH,
    )

    def meet():
        pl.semaphore_wait(barrier, peers)
        repeat(ny, send_part)

    early = mx == 0
    pl.when(jnp.logical_not(early))(meet)

    loads[4].wait()
    depth = (sea * lay_v[...]).astype(jnp.float32)
    depth_v[...] = depth

    half = h // 2
    depth_at = 6 * nk
    lane = lax.broadcasted_iota(jnp.int32, (h, w), 1)
    row = lax.broadcasted_iota(jnp.int32, (h, w), 0)
    slot = jnp.where(row < half, lane, lane - 1)
    pair = slot >> 1
    eastern = (slot & 1) == 0
    even_half = (lane[:half] & 1) == 0

    def spread(plane, j):
        return jnp.concatenate(
            [pltpu.roll(plane[:half], 2 * j + 1, 1), pltpu.roll(plane[half:], 2 * j + 2, 1)], axis=0
        )

    packed = jnp.where(pair == 3 * nk, spread(depth, 3 * nk), 0.0)
    for i, (load, ref) in enumerate(zip(loads[5:8], (t_v, s_v, uv_v))):
        load.wait()
        for k in range(nk):
            j = i * nk + k
            packed = jnp.where(pair == j, spread(ref[pl.ds(k * h, h), :], j), packed)
    last_v[...] = jnp.where(even_half, packed[:half], packed[half:])
    first_v[...] = jnp.where(even_half, packed[half:], packed[:half])

    to_east = pltpu.make_async_remote_copy(
        src_ref=last_v, dst_ref=west_v, send_sem=pack_send.at[0], recv_sem=pack_recv.at[0],
        device_id={"gx": lax.rem(mx + 1, nx)}, device_id_type=MESH,
    )
    to_west = pltpu.make_async_remote_copy(
        src_ref=first_v, dst_ref=east_v, send_sem=pack_send.at[1], recv_sem=pack_recv.at[1],
        device_id={"gx": lax.rem(mx + nx - 1, nx)}, device_id_type=MESH,
    )
    depth_east = jnp.where(lane == w - 1, 0.0, jnp.minimum(depth, pltpu.roll(depth, w - 1, 1)))
    depth_north = jnp.where(row == h - 1, 0.0, jnp.minimum(depth, pltpu.roll(depth, h - 1, 0)))

    def level(k, above):
        kf = k.astype(jnp.float32)
        at = pl.ds(pl.multiple_of(k * h, h), h)
        below = pl.ds(pl.multiple_of(jnp.minimum(k + 1, nk - 1) * h, h), h)
        east_near, east_far = face_weights(uv_v[at, :], depth_east > kf)
        north_near, north_far = face_weights(
            uv_v[pl.ds(pl.multiple_of((k + nk) * h, h), h), :], depth_north > kf
        )
        mix = jnp.where(depth_v[...] > kf + 1.0, time_step * vertical_mixing, 0.0)
        gain = g_v[...]
        falls = []
        for ref, out, came in ((t_v, t_out, above[0]), (s_v, s_out, above[1])):
            c = ref[at, :]
            east = east_near * c + east_far * pltpu.roll(c, w - 1, 1)
            north = north_near * c + north_far * pltpu.roll(c, h - 1, 0)
            flow = (pltpu.roll(east, 1, 1) - east) + (pltpu.roll(north, 1, 0) - north)
            fall = mix * (c - ref[below, :])
            out[at, :] = c + (gain * flow + (came - fall))
            falls.append(fall)
        return tuple(falls)

    zero = jnp.zeros((h, w), jnp.float32)
    pack_v[...] = packed
    split = jnp.where(early, nk, 0)

    @pl.when(early)
    def _():
        for load in loads[8:]:
            load.wait()

    falls = lax.fori_loop(0, split, level, (zero, zero))
    pl.when(early)(meet)
    to_east.start()
    to_west.start()
    repeat(peers - ny + 1, lambda r: send_part(r + ny))

    @pl.when(jnp.logical_not(early))
    def _():
        for load in loads[8:]:
            load.wait()


    def rows(ref, row, base=0):
        return ref[pl.ds(base + row, nk, stride=h), :]

    up_v[pl.ds(0, nk), :] = rows(t_v, h - 1)
    up_v[pl.ds(nk, nk), :] = rows(s_v, h - 1)
    up_v[pl.ds(2 * nk, nk), :] = rows(uv_v, h - 1, nk * h)
    up_v[pl.ds(3 * nk, 8), :] = jnp.broadcast_to(depth[h - 1 : h, :], (8, w))
    down_v[pl.ds(0, nk), :] = rows(t_v, 0)
    down_v[pl.ds(nk, nk), :] = rows(s_v, 0)
    down_v[pl.ds(2 * nk, 8), :] = jnp.broadcast_to(depth[0:1, :], (8, w))

    @pl.when(is_top)
    def _():
        up = up_v[...]
        flip = (w - 1) - lax.broadcasted_iota(jnp.int32, up.shape, 1)
        fold_v[mx] = jnp.take_along_axis(up, flip, axis=1)

    to_north = pltpu.make_async_remote_copy(
        src_ref=up_v, dst_ref=south_v, send_sem=row_send.at[0], recv_sem=row_recv.at[0],
        device_id={"gy": lax.rem(my + 1, ny)}, device_id_type=MESH,
    )
    to_south = pltpu.make_async_remote_copy(
        src_ref=down_v, dst_ref=north_v, send_sem=row_send.at[1], recv_sem=row_recv.at[1],
        device_id={"gy": lax.rem(my + ny - 1, ny)}, device_id_type=MESH,
    )

    def fold_copy(d):
        return pltpu.make_async_remote_copy(
            src_ref=fold_v.at[mx], dst_ref=fold_v.at[mx],
            send_sem=fold_send.at[d], recv_sem=fold_recv.at[d],
            device_id={"gx": lax.rem(mx + d + 1, nx)}, device_id_type=MESH,
        )


    @pl.when(jnp.logical_not(is_top))
    def _():
        to_north.start()

    @pl.when(my > 0)
    def _():
        to_south.start()

    @pl.when(is_top)
    def _():
        repeat(nx - 1, lambda d: fold_copy(d).start())

    lax.fori_loop(split, nk, level, falls)

    level_row = lax.broadcasted_iota(jnp.int32, (nk, w), 0).astype(jnp.float32)

    def north_edge(far_t, far_s, speed, far_depth):
        near_weight, far_weight = face_weights(
            speed, jnp.minimum(up_v[3 * nk : 3 * nk + 1, :], far_depth) > level_row
        )
        for near, far, out in (
            (up_v[pl.ds(0, nk), :], far_t, t_out),
            (up_v[pl.ds(nk, nk), :], far_s, s_out),
        ):
            at = pl.ds(h - 1, nk, stride=h)
            out[at, :] -= g_v[h - 1 : h, :] * (near_weight * near + far_weight * far)

    @pl.when(jnp.logical_not(is_top))
    def _():
        to_north.wait_send()
        to_south.wait_recv()
        north_edge(
            north_v[pl.ds(0, nk), :],
            north_v[pl.ds(nk, nk), :],
            up_v[pl.ds(2 * nk, nk), :],
            north_v[2 * nk : 2 * nk + 1, :],
        )

    @pl.when(my > 0)
    def _():
        to_south.wait_send()
        to_north.wait_recv()
        near_weight, far_weight = face_weights(
            south_v[pl.ds(2 * nk, nk), :],
            jnp.minimum(down_v[2 * nk : 2 * nk + 1, :], south_v[3 * nk : 3 * nk + 1, :]) > level_row,
        )
        for i, out in enumerate((t_out, s_out)):
            at = pl.ds(0, nk, stride=h)
            out[at, :] += g_v[0:1, :] * (
                near_weight * south_v[pl.ds(i * nk, nk), :]
                + far_weight * down_v[pl.ds(i * nk, nk), :]
            )

    @pl.when(is_top)
    def _():
        repeat(nx - 1, lambda d: fold_copy(d).wait())
        partner = fold_v[seam_smem[0] // w]
        north_edge(
            partner[:nk],
            partner[nk : 2 * nk],
            0.5 * (up_v[pl.ds(2 * nk, nk), :] - partner[2 * nk : 3 * nk]),
            partner[3 * nk : 3 * nk + 1],
        )

    all_parts.wait()
    totals = jnp.sum(parts_v[...], axis=0)
    total_area, total_fresh, salt_fresh, salt_only = (
        jnp.broadcast_to(totals[:, i : i + 1], (1, w)) for i in range(4)
    )
    mean_fresh = total_fresh / total_area
    lift = (salt_fresh - mean_fresh * salt_only) / total_area
    virtual = lift - s0_v[...] * (rain_v[...] - mean_fresh)
    s_out[pl.ds(0, h), :] += jnp.where(depth_v[...] > 0.0, time_step / top_thickness * virtual, 0.0)

    def column(cells, upper, lower):
        return jnp.concatenate(
            [
                jnp.broadcast_to(cells[:half, upper : upper + 1], (half, w)),
                jnp.broadcast_to(cells[-half:, lower : lower + 1], (half, w)),
            ],
            axis=0,
        )

    def both(cells):
        return jnp.concatenate([cells, cells], axis=0)

    def speeds(cells, shift):
        return (
            pltpu.roll(cells, (shift + w - 4 * nk) % w, 1),
            pltpu.roll(cells, (shift + w - 2 * nk) % w, 1),
        )

    mine = pack_v[...]
    own_t, own_s = speeds(mine, 0)
    depth = depth_v[...]
    own_depth = jnp.where(eastern, column(depth, w - 1, w - 1), column(depth, 0, 0))
    gain = g_v[...]
    edge_gain = jnp.where(eastern, -column(gain, w - 1, w - 1), column(gain, 0, 0))
    edge_gain = jnp.where(own_depth > (pair & (nk - 1)).astype(jnp.float32), edge_gain, 0.0)

    to_east.wait()
    to_west.wait()
    west, east = west_v[...], east_v[...]
    west_t, west_s = speeds(west, 1)
    near = jnp.where(eastern, mine, both(pltpu.roll(west, 1, 1)))
    far = jnp.where(eastern, both(pltpu.roll(east, w - 1, 1)), mine)
    speed = jnp.where(
        eastern,
        jnp.where(pair < nk, own_t, own_s),
        jnp.where(pair < nk, both(west_t), both(west_s)),
    )
    far_depth = jnp.where(
        eastern,
        column(east, depth_at + 1, depth_at + 2),
        column(west, depth_at, depth_at + 1),
    )
    near_weight, far_weight = face_weights(
        speed, far_depth > (pair & (nk - 1)).astype(jnp.float32)
    )
    edge_out[...] = edge_gain * (near_weight * near + far_weight * far)


store_cuts = 4


def store_kernel(nk, h, w, t_ref, s_ref, edge_ref, t_hbm, s_hbm, t_v, s_v, sems):
    half = h // 2
    lane = lax.broadcasted_iota(jnp.int32, (half, w), 1)
    at_edge = (lane == 0) | (lane == w - 1)
    step = nk // store_cuts
    copies = []
    for i, (ref, out, hbm) in enumerate(((t_ref, t_v, t_hbm), (s_ref, s_v, s_hbm))):
        for cut in range(store_cuts):
            for k in range(cut * step, (cut + 1) * step):
                j = i * nk + k
                for part, shift in ((0, w - 1 - 2 * j), (1, w - 2 - 2 * j)):
                    moved = pltpu.roll(edge_ref[pl.ds(part * half, half), :], shift % w, 1)
                    at = pl.ds(k * h + part * half, half)
                    out[at, :] = ref[at, :] + jnp.where(at_edge, moved, 0.0)
            at = pl.ds(cut * step * h, step * h)
            copy = pltpu.make_async_copy(out.at[at], hbm.at[at], sems.at[len(copies)])
            copy.start()
            copies.append(copy)
    for copy in copies:
        copy.wait()


def shards(nx, ny, t, s, uv, sea, layers, area, rain, seam):
    nk, h, w = t.shape
    assert w == 128 and h % 16 == 0 and nk & (nk - 1) == 0 and nk % 8 == 0 and 6 * nk + 3 <= w
    f32 = jnp.float32
    peers = nx * ny - 1
    half_plane = pltpu.VMEM((h // 2, w), f32)
    any_space = pl.BlockSpec(memory_space=pl.ANY)
    dma = pltpu.SemaphoreType.DMA
    plane = pltpu.VMEM((h, w), f32)
    t_next, s_next, edge = pl.pallas_call(
        functools.partial(kernel, nx, ny, nk, h, w),
        out_shape=[pltpu.VMEM((nk * h, w), f32)] * 2 + [pltpu.VMEM((h, w), f32)],
        in_specs=[any_space] * 8,
        out_specs=[pl.BlockSpec(memory_space=pltpu.VMEM)] * 3,
        scratch_shapes=[
            pltpu.VMEM((nk * h, w), f32),
            pltpu.VMEM((nk * h, w), f32),
            pltpu.VMEM((2 * nk * h, w), f32),
            pltpu.VMEM((h, w), jnp.int32),
            pltpu.VMEM((h, w), jnp.int32),
            plane, plane, plane, plane, plane,
            plane, half_plane, half_plane, half_plane, half_plane,
            pltpu.VMEM((3 * nk + 8, w), f32),
            pltpu.VMEM((2 * nk + 8, w), f32),
            pltpu.VMEM((3 * nk + 8, w), f32),
            pltpu.VMEM((2 * nk + 8, w), f32),
            pltpu.VMEM((nx, 3 * nk + 8, w), f32),
            pltpu.VMEM((1, w), f32),
            pltpu.VMEM((nx * ny, 1, w), f32),
            pltpu.SMEM((w,), jnp.int32),
            dma((10,)), dma((2,)), dma((2,)), dma((2,)), dma((2,)),
            dma((nx - 1,)), dma((nx - 1,)), dma, dma,
        ],
        compiler_params=pltpu.CompilerParams(
            collective_id=0, has_side_effects=True, vmem_limit_bytes=65961984
        ),
        name="tracer_step",
    )(
        t.reshape(nk * h, w), s.reshape(nk * h, w), uv.reshape(2 * nk * h, w),
        sea, layers, area, rain, seam,
    )
    t_next, s_next = pl.pallas_call(
        functools.partial(store_kernel, nk, h, w),
        out_shape=[jax.ShapeDtypeStruct((nk * h, w), f32)] * 2,
        in_specs=[pl.BlockSpec(memory_space=pltpu.VMEM)] * 3,
        out_specs=[any_space] * 2,
        scratch_shapes=[pltpu.VMEM((nk * h, w), f32)] * 2 + [dma((2 * store_cuts,))],
        compiler_params=pltpu.CompilerParams(vmem_limit_bytes=8 << 20),
        name="store",
    )(t_next, s_next, edge)
    return t_next.reshape(t.shape), s_next.reshape(s.shape)


def solution(mesh):
    in_specs = (
        P("groups", "gy", "gx"),
        P("groups", "gy", "gx"),
        P("groups", None, "gy", "gx"),
        P("gy", "gx"),
        P("gy", "gx"),
        P("gy", "gx"),
        P("gy", "gx"),
        P("gx"),
    )
    out_specs = (P("groups", "gy", "gx"), P("groups", "gy", "gx"))
    return jax.shard_map(
        functools.partial(shards, mesh.shape["gx"], mesh.shape["gy"]),
        mesh=mesh, in_specs=in_specs, out_specs=out_specs, check_vma=False,
    )
```

time: 12.4 us -> 11.5 us (0.927)
  Pallas kernels: 11.6 us -> 10.7 us
    pallas_call x1, Pallas kernels: 10.6 us -> 9.56 us  [shards(): pl.pallas_call(functools.partial(kernel, nx, ny, nk, h, w), out_shape=[pl...]
    pallas_call x1, Pallas kernels: 0.99 us -> 1.13 us  [shards(): pl.pallas_call(functools.partial(store_kernel, nk, h, w), out_shape=[jax....]
where the time goes in v1:
time: 11.5 us; the launch traced here: 11.3 us
  Pallas kernels  10.7 us (93%)
  between operations  0.64 us (6%)
    pallas_call x1, Pallas kernels, shards(): pl.pallas_call(functools.partial(kernel, nx, ny, nk, h, w), out_shape=[pl...  9.56 us
    pallas_call x1, Pallas kernels, shards(): pl.pallas_call(functools.partial(store_kernel, nk, h, w), out_shape=[jax....  1.13 us

profile of v1, /device:TPU:0, one launch (start us, length us, event | category | flops | bytes accessed | tf_op | source)
XLA Modules:
  0.0 11.3 jit_solution(5219156019842474231)
XLA Ops:
  0.6 9.6 %tracer_step.1 = (f32[1024,128]{1,0:T(8,128)S(1)}, f32[1024,128]{1,0:T(8,128)S(1)}, f32[64,128]{1,0:T(8,128)S(1)}) custom-call(f32[1024,128]{1,0:T(8,128)} %bitcast.6, f32[1024,128]{1,0:T(8,128)} %bitcast.7, f32[2048,128]{1,0:T(8,128)} %bitcast.5, s32[64,128]{1,0:T(8,128)} %sea_hbm.1, s32[64,128]{1,0:T(8,128)} %lay_hbm.1, f32[64,128]{1,0:T(8,128)} %area_hbm.1, ...), custom_call_target="tpu_custom_call" | custom-call | tf_op jit(solution)/shard_map/tracer_step/pallas_call | solution.py:390
  10.2 1.1 %store.1 = (f32[1024,128]{1,0:T(8,128)}, f32[1024,128]{1,0:T(8,128)}) custom-call(f32[1024,128]{1,0:T(8,128)S(1)} %get-tuple-element.7.t_ref, f32[1024,128]{1,0:T(8,128)S(1)} %get-tuple-element.8.s_ref, f32[64,128]{1,0:T(8,128)S(1)} %get-tuple-element.9.edge_ref), custom_call_target="tpu_custom_call" | custom-call | tf_op jit(solution)/shard_map/store/pallas_call | solution.py:422

commit v2 on v1

v2 whole, which is shorter than its diff:
```python
import functools

import jax
import jax.numpy as jnp
from jax import lax
from jax.experimental import pallas as pl
from jax.experimental.pallas import tpu as pltpu
from jax.sharding import PartitionSpec as P

time_step = 0.25
diffusivity = 0.5
vertical_mixing = 0.3
top_thickness = 0.5

block_rows = 16
hubs = 2

MESH = pl.DeviceIdType.MESH


def repeat(count, body):
    if count <= 16:
        for i in range(count):
            body(i)
    else:
        pl.loop(0, count)(body)


def face_weights(speed, open_face):
    near_weight = jnp.maximum(speed, 0.0) + diffusivity
    far_weight = speed - near_weight
    return jnp.where(open_face, near_weight, 0.0), jnp.where(open_face, far_weight, 0.0)


def kernel(
    nx, ny, nk, h, w,
    t_hbm, s_hbm, uv_hbm, sea_hbm, lay_hbm, area_hbm, rain_hbm, seam_hbm,
    t_out, s_out, side_out,
    t_v, s_v, uv_v, sea_v, lay_v, area_v, rain_v, s0_v, g_v, depth_v,
    pack_v, last_v, first_v, east_v, west_v, up_v, down_v, south_v, north_v, fold_v,
    part_v, parts_v, total_v, seam_smem, depth_east_v, depth_north_v, flux_v,
    load_sems, pack_send, pack_recv, row_send, row_recv, fold_send, fold_recv,
    part_send, part_recv, total_send, total_recv,
):
    mx, my = lax.axis_index("gx"), lax.axis_index("gy")
    is_top = my == ny - 1
    peers = nx * ny - 1

    barrier = pltpu.get_barrier_semaphore()

    east, west = lax.rem(mx + 1, nx), lax.rem(mx + nx - 1, nx)
    is_hub = mx < hubs
    outside = jnp.logical_not(is_hub)

    def count(flag):
        return jnp.where(flag, 1, 0)

    far_sides = count(east >= hubs) + count(west >= hubs)
    partners = (
        hubs * ny - count(is_hub) + far_sides
        + jnp.where(outside, count(my > 0) + count(my < ny - 1), 0)
        + jnp.where(is_top, nx - hubs - count(outside) - far_sides, 0)
    )

    def signal(gx, gy):
        pl.semaphore_signal(
            barrier, inc=1, device_id={"gx": gx, "gy": gy}, device_id_type=MESH
        )

    def greet():
        @pl.when(is_hub)
        def _():
            def one(r):
                r = r + 1
                signal(lax.rem(mx + r // ny, nx), lax.rem(my + r % ny, ny))

            repeat(peers, one)

        @pl.when(outside)
        def _():
            signal(west, my)
            signal(east, my)
            pl.when(my > 0)(lambda: signal(mx, my - 1))
            pl.when(my < ny - 1)(lambda: signal(mx, my + 1))

        @pl.when(outside & is_top)
        def _():
            repeat(nx - 3, lambda d: signal(lax.rem(mx + 2 + d, nx), my))

    loads = [
        pltpu.make_async_copy(src, dst, load_sems.at[i])
        for i, (src, dst) in enumerate(
            [
                (area_hbm, area_v),
                (sea_hbm, sea_v),
                (rain_hbm, rain_v),
                (s_hbm.at[pl.ds(0, h)], s0_v),
                (lay_hbm, lay_v),
                (t_hbm, t_v.at[pl.ds(0, nk * h)]),
                (s_hbm, s_v.at[pl.ds(0, nk * h)]),
                (uv_hbm.at[pl.ds(0, nk * h)], uv_v.at[pl.ds(0, nk * h)]),
                (uv_hbm.at[pl.ds(nk * h, nk * h)], uv_v.at[pl.ds(nk * h, nk * h)]),
                (seam_hbm, seam_smem),
            ]
        )
    ]
    for load in loads[:8]:
        load.start()
    greet()
    for load in loads[8:]:
        load.start()
    zeros = jnp.zeros((8, w), jnp.float32)
    for ref in (t_v, s_v):
        ref[pl.ds(nk * h, 8), :] = zeros
    for i in range(2 * nk):
        flux_v[pl.ds(i * (h + 8), 8), :] = zeros

    for load in loads[:4]:
        load.wait()
    area = area_v[...]
    sea = sea_v[...]
    wet_area = area * sea.astype(jnp.float32)
    surface = s0_v[...]
    fresh = wet_area * rain_v[...]
    lane1 = lax.broadcasted_iota(jnp.int32, (1, w), 1)
    part = jnp.zeros((1, w), jnp.float32)
    for i, term in enumerate((wet_area, fresh, fresh * surface, wet_area * surface)):
        rows8 = jnp.sum(term.reshape(h // 8, 8, w), axis=0)
        part = jnp.where(
            lane1 == i, jnp.sum(jnp.sum(rows8, axis=1, keepdims=True), axis=0, keepdims=True), part
        )
    part_v[...] = part
    gain = time_step / area
    g_v[...] = gain

    me = mx * ny + my
    parts_v[me] = part

    def send_part(r):
        @pl.when(r != me)
        def _():
            pltpu.make_async_remote_copy(
                src_ref=part_v, dst_ref=parts_v.at[me], send_sem=part_send, recv_sem=part_recv,
                device_id={"gx": r // ny, "gy": r % ny}, device_id_type=MESH,
            ).start()

    def several(ref, n, sends, arrivals):
        block = ref.at[pl.ds(0, n)]
        return pltpu.make_async_remote_copy(
            src_ref=block, dst_ref=block, send_sem=sends, recv_sem=arrivals,
            device_id={"gx": east}, device_id_type=MESH,
        )

    def hand_on(d):
        return pltpu.make_async_remote_copy(
            src_ref=total_v, dst_ref=total_v, send_sem=total_send, recv_sem=total_recv,
            device_id={"gx": hubs + d}, device_id_type=MESH,
        )

    def meet():
        pl.semaphore_wait(barrier, partners)
        repeat(hubs * ny, send_part)

    early = mx == 0
    pl.when(jnp.logical_not(early))(meet)

    loads[4].wait()
    depth = (sea * lay_v[...]).astype(jnp.float32)
    depth_v[...] = depth

    half = h // 2
    depth_at = 6 * nk
    lane = lax.broadcasted_iota(jnp.int32, (h, w), 1)
    row = lax.broadcasted_iota(jnp.int32, (h, w), 0)
    slot = jnp.where(row < half, lane, lane - 1)
    pair = slot >> 1
    eastern = (slot & 1) == 0
    even_half = (lane[:half] & 1) == 0

    quarter = h // 4

    def cells(ref, k, b):
        return [
            ref[pl.ds(k * h + side * half + b * quarter, quarter), :] for side in (0, 1)
        ]

    def pack(packed, b, ref, first, count):
        for k in range(count):
            j = first + k
            packed = [
                jnp.where(
                    pair[side * half : side * half + quarter] == j,
                    pltpu.roll(plane, 2 * j + 1 + side, 1),
                    old,
                )
                for side, (plane, old) in enumerate(zip(cells(ref, k, b), packed))
            ]
        return packed

    empty = [jnp.zeros((quarter, w), jnp.float32)] * 2
    packed = [pack(empty, b, depth_v, 3 * nk, 1) for b in (0, 1)]
    for i, ref in enumerate((t_v, s_v)):
        loads[5 + i].wait()
        packed = [pack(packed[b], b, ref, i * nk, nk) for b in (0, 1)]
    loads[7].wait()

    def finish(b):
        upper, lower = pack(packed[b], b, uv_v, 2 * nk, nk)
        pack_v[pl.ds(b * quarter, quarter), :] = upper
        pack_v[pl.ds(half + b * quarter, quarter), :] = lower
        at = pl.ds(b * quarter, quarter)
        last_v[at, :] = jnp.where(even_half[:quarter], upper, lower)
        first_v[at, :] = jnp.where(even_half[:quarter], lower, upper)

    def strip(b, src, dst, n, step):
        at = pl.ds(b * quarter, quarter)
        return pltpu.make_async_remote_copy(
            src_ref=src.at[at], dst_ref=dst.at[at],
            send_sem=pack_send.at[2 * b + n], recv_sem=pack_recv.at[2 * b + n],
            device_id={"gx": lax.rem(mx + step, nx)}, device_id_type=MESH,
        )

    to_east = [strip(b, last_v, west_v, 0, 1) for b in (0, 1)]
    to_west = [strip(b, first_v, east_v, 1, nx - 1) for b in (0, 1)]

    for b in (0, 1):
        finish(b)
        pl.when(jnp.logical_not(early))(to_east[b].start)

    depth_east_v[...] = jnp.where(
        lane == w - 1, 0.0, jnp.minimum(depth, pltpu.roll(depth, w - 1, 1))
    )
    depth_north_v[...] = jnp.where(
        row == h - 1, 0.0, jnp.minimum(depth, pltpu.roll(depth, h - 1, 0))
    )

    def interior(block, carry):
        start = pl.multiple_of(block * block_rows, block_rows)
        here = pl.ds(start, block_rows)
        deep_east, deep_north = depth_east_v[here, :], depth_north_v[here, :]
        deep, gain = depth_v[here, :], g_v[here, :]
        came = [0.0, 0.0]
        for k in range(nk):
            at = pl.ds(start + k * h, block_rows)
            east_near, east_far = face_weights(uv_v[at, :], deep_east > k)
            north_near, north_far = face_weights(
                uv_v[pl.ds(start + (nk + k) * h, block_rows), :], deep_north > k
            )
            mix = jnp.where(deep > k + 1, time_step * vertical_mixing, 0.0)
            for n, (ref, out) in enumerate(((t_v, t_out), (s_v, s_out))):
                c = ref[at, :]
                east = east_near * c + east_far * pltpu.roll(c, w - 1, 1)
                north = north_near * c + north_far * ref[pl.ds(start + k * h + 1, block_rows), :]
                strip_at = (n * nk + k) * (h + 8) + 8
                flux_v[pl.ds(start + strip_at, block_rows), :] = north
                south = flux_v[pl.ds(start + strip_at - 1, block_rows), :]
                flow = (pltpu.roll(east, 1, 1) - east) + (south - north)
                fall = 0.0
                if k < nk - 1:
                    fall = mix * (c - ref[pl.ds(start + (k + 1) * h, block_rows), :])
                out[at, :] = c + (gain * flow + (came[n] - fall))
                came[n] = fall
        return carry

    split = jnp.where(early, h // block_rows, 0)

    @pl.when(early)
    def _():
        for load in loads[8:]:
            load.wait()

    lax.fori_loop(0, split, interior, 0)
    pl.when(early)(meet)

    @pl.when(early)
    def _():
        for b in (0, 1):
            to_east[b].start()

    for b in (0, 1):
        to_west[b].start()
    @pl.when(jnp.logical_not(early))
    def _():
        for load in loads[8:]:
            load.wait()


    def rows(ref, row, base=0):
        return ref[pl.ds(base + row, nk, stride=h), :]

    up_v[pl.ds(0, nk), :] = rows(t_v, h - 1)
    up_v[pl.ds(nk, nk), :] = rows(s_v, h - 1)
    up_v[pl.ds(2 * nk, nk), :] = rows(uv_v, h - 1, nk * h)
    up_v[pl.ds(3 * nk, 8), :] = jnp.broadcast_to(depth[h - 1 : h, :], (8, w))
    down_v[pl.ds(0, nk), :] = rows(t_v, 0)
    down_v[pl.ds(nk, nk), :] = rows(s_v, 0)
    down_v[pl.ds(2 * nk, 8), :] = jnp.broadcast_to(depth[0:1, :], (8, w))

    @pl.when(is_top)
    def _():
        up = up_v[...]
        flip = (w - 1) - lax.broadcasted_iota(jnp.int32, up.shape, 1)
        fold_v[mx] = jnp.take_along_axis(up, flip, axis=1)

    to_north = pltpu.make_async_remote_copy(
        src_ref=up_v, dst_ref=south_v, send_sem=row_send.at[0], recv_sem=row_recv.at[0],
        device_id={"gy": lax.rem(my + 1, ny)}, device_id_type=MESH,
    )
    to_south = pltpu.make_async_remote_copy(
        src_ref=down_v, dst_ref=north_v, send_sem=row_send.at[1], recv_sem=row_recv.at[1],
        device_id={"gy": lax.rem(my + ny - 1, ny)}, device_id_type=MESH,
    )

    def fold_copy(d):
        return pltpu.make_async_remote_copy(
            src_ref=fold_v.at[mx], dst_ref=fold_v.at[mx],
            send_sem=fold_send.at[d], recv_sem=fold_recv.at[d],
            device_id={"gx": lax.rem(mx + d + 1, nx)}, device_id_type=MESH,
        )


    @pl.when(jnp.logical_not(is_top))
    def _():
        to_north.start()

    @pl.when(my > 0)
    def _():
        to_south.start()

    @pl.when(is_top)
    def _():
        repeat(nx - 1, lambda d: fold_copy(d).start())

    lax.fori_loop(split, h // block_rows, interior, 0)

    level_row = lax.broadcasted_iota(jnp.int32, (nk, w), 0).astype(jnp.float32)

    def north_edge(far_t, far_s, speed, far_depth):
        near_weight, far_weight = face_weights(
            speed, jnp.minimum(up_v[3 * nk : 3 * nk + 1, :], far_depth) > level_row
        )
        for near, far, out in (
            (up_v[pl.ds(0, nk), :], far_t, t_out),
            (up_v[pl.ds(nk, nk), :], far_s, s_out),
        ):
            at = pl.ds(h - 1, nk, stride=h)
            out[at, :] -= g_v[h - 1 : h, :] * (near_weight * near + far_weight * far)

    @pl.when(jnp.logical_not(is_top))
    def _():
        to_north.wait_send()
        to_south.wait_recv()
        north_edge(
            north_v[pl.ds(0, nk), :],
            north_v[pl.ds(nk, nk), :],
            up_v[pl.ds(2 * nk, nk), :],
            north_v[2 * nk : 2 * nk + 1, :],
        )

    @pl.when(my > 0)
    def _():
        to_south.wait_send()
        to_north.wait_recv()
        near_weight, far_weight = face_weights(
            south_v[pl.ds(2 * nk, nk), :],
            jnp.minimum(down_v[2 * nk : 2 * nk + 1, :], south_v[3 * nk : 3 * nk + 1, :]) > level_row,
        )
        for i, out in enumerate((t_out, s_out)):
            at = pl.ds(0, nk, stride=h)
            out[at, :] += g_v[0:1, :] * (
                near_weight * south_v[pl.ds(i * nk, nk), :]
                + far_weight * down_v[pl.ds(i * nk, nk), :]
            )

    @pl.when(is_hub)
    def _():
        several(parts_v, peers, part_send, part_recv).wait_recv()
        total_v[...] = jnp.sum(parts_v[...], axis=0)

    @pl.when(mx == hubs - 1)
    def _():
        repeat(nx - hubs, lambda d: hand_on(d).start())

    @pl.when(is_top)
    def _():
        repeat(nx - 1, lambda d: fold_copy(d).wait())
        partner = fold_v[seam_smem[0] // w]
        north_edge(
            partner[:nk],
            partner[nk : 2 * nk],
            0.5 * (up_v[pl.ds(2 * nk, nk), :] - partner[2 * nk : 3 * nk]),
            partner[3 * nk : 3 * nk + 1],
        )

    def column(plane, at):
        return jnp.broadcast_to(plane[:, at : at + 1], (h, w))

    mine = pack_v[...]
    depth = depth_v[...]
    gain = g_v[...]
    level_of = (pair & (nk - 1)).astype(jnp.float32)
    open_cell = jnp.where(eastern, column(depth, w - 1), column(depth, 0)) > level_of
    edge_gain = jnp.where(eastern, -column(gain, w - 1), column(gain, 0))
    surface_wet = jnp.where(depth > 0.0, time_step / top_thickness, 0.0)
    surface = s0_v[...]
    s_out[pl.ds(0, h), :] -= surface_wet * surface * rain_v[...]
    for i, plane in enumerate(
        (
            mine,
            jnp.where(pair < nk, pltpu.roll(mine, w - 4 * nk, 1), pltpu.roll(mine, w - 2 * nk, 1)),
            jnp.where(open_cell, edge_gain, 0.0),
            surface_wet * surface,
            surface_wet,
        )
    ):
        side_out[pl.ds(i * h, h), :] = plane

    @pl.when(is_hub)
    def _():
        several(parts_v, hubs * ny - 1, part_send, part_recv).wait_send()

    @pl.when(outside)
    def _():
        several(parts_v, hubs * ny, part_send, part_recv).wait_send()
        hand_on(0).wait_recv()

    @pl.when(mx == hubs - 1)
    def _():
        several(parts_v, nx - hubs, total_send, total_recv).wait_send()

    side_out[pl.ds(6 * h, 8), :] = jnp.broadcast_to(total_v[...], (8, w))
    for b in (0, 1):
        to_east[b].wait()
        to_west[b].wait()
    side_out[pl.ds(5 * h, half), :] = west_v[...]
    side_out[pl.ds(5 * h + half, half), :] = east_v[...]


store_cuts = 4


def store_kernel(nk, h, w, t_ref, s_ref, side_ref, t_hbm, s_hbm, t_v, s_v, sems):
    half = h // 2
    mine, own_speed, edge_gain, surface, surface_wet = (
        side_ref[pl.ds(i * h, h), :] for i in range(5)
    )
    west = side_ref[pl.ds(5 * h, half), :]
    east = side_ref[pl.ds(5 * h + half, half), :]
    totals = side_ref[pl.ds(6 * h, 1), :]

    lane = lax.broadcasted_iota(jnp.int32, (h, w), 1)
    slot = jnp.where(lax.broadcasted_iota(jnp.int32, (h, w), 0) < half, lane, lane - 1)
    pair = slot >> 1
    eastern = (slot & 1) == 0

    def both(cells):
        return jnp.concatenate([cells, cells], axis=0)

    def moved(cells, by):
        return both(pltpu.roll(cells, by % w, 1))

    def columns(cells, at):
        return jnp.concatenate(
            [jnp.broadcast_to(cells[:, i : i + 1], (half, w)) for i in (at, at + 1)], axis=0
        )

    near = jnp.where(eastern, mine, moved(west, 1))
    far = jnp.where(eastern, moved(east, -1), mine)
    west_speed = jnp.where(pair < nk, moved(west, 1 - 4 * nk), moved(west, 1 - 2 * nk))
    far_depth = jnp.where(eastern, columns(east, 6 * nk + 1), columns(west, 6 * nk))
    near_weight, far_weight = face_weights(
        jnp.where(eastern, own_speed, west_speed),
        far_depth > (pair & (nk - 1)).astype(jnp.float32),
    )
    edge = edge_gain * (near_weight * near + far_weight * far)

    total_area, total_fresh, salt_fresh, salt_only = (
        jnp.broadcast_to(totals[:, i : i + 1], (1, w)) for i in range(4)
    )
    mean_fresh = total_fresh / total_area
    lift = (salt_fresh - mean_fresh * salt_only) / total_area
    virtual = surface_wet * lift + surface * mean_fresh

    at_edge = (lane[:half] == 0) | (lane[:half] == w - 1)
    step = nk // store_cuts
    copies = []
    for i, (ref, out, hbm) in enumerate(((t_ref, t_v, t_hbm), (s_ref, s_v, s_hbm))):
        for cut in reversed(range(store_cuts)):
            for k in range(cut * step, (cut + 1) * step):
                j = i * nk + k
                for part, shift in ((0, w - 1 - 2 * j), (1, w - 2 - 2 * j)):
                    rows = slice(part * half, (part + 1) * half)
                    change = jnp.where(at_edge, pltpu.roll(edge[rows], shift % w, 1), 0.0)
                    if j == nk:
                        change = change + virtual[rows]
                    at = pl.ds(k * h + part * half, half)
                    out[at, :] = ref[at, :] + change
            at = pl.ds(cut * step * h, step * h)
            copy = pltpu.make_async_copy(out.at[at], hbm.at[at], sems.at[len(copies)])
            copy.start()
            copies.append(copy)
    for copy in copies:
        copy.wait()


def shards(nx, ny, t, s, uv, sea, layers, area, rain, seam):
    nk, h, w = t.shape
    assert w == 128 and h % 16 == 0 and nk & (nk - 1) == 0 and nk % 8 == 0 and 6 * nk + 3 <= w and nx > 3 and hubs == 2
    f32 = jnp.float32
    peers = nx * ny - 1
    half_plane = pltpu.VMEM((h // 2, w), f32)
    vmem = 67043328 - 4 * w * (2 * nk * h + 6 * h + 8)
    any_space = pl.BlockSpec(memory_space=pl.ANY)
    dma = pltpu.SemaphoreType.DMA
    plane = pltpu.VMEM((h, w), f32)
    t_next, s_next, side = pl.pallas_call(
        functools.partial(kernel, nx, ny, nk, h, w),
        out_shape=[pltpu.VMEM((nk * h, w), f32)] * 2 + [pltpu.VMEM((6 * h + 8, w), f32)],
        in_specs=[any_space] * 8,
        out_specs=[pl.BlockSpec(memory_space=pltpu.VMEM)] * 3,
        scratch_shapes=[
            pltpu.VMEM((nk * h + 8, w), f32),
            pltpu.VMEM((nk * h + 8, w), f32),
            pltpu.VMEM((2 * nk * h, w), f32),
            pltpu.VMEM((h, w), jnp.int32),
            pltpu.VMEM((h, w), jnp.int32),
            plane, plane, plane, plane, plane,
            plane, half_plane, half_plane, half_plane, half_plane,
            pltpu.VMEM((3 * nk + 8, w), f32),
            pltpu.VMEM((2 * nk + 8, w), f32),
            pltpu.VMEM((3 * nk + 8, w), f32),
            pltpu.VMEM((2 * nk + 8, w), f32),
            pltpu.VMEM((nx, 3 * nk + 8, w), f32),
            pltpu.VMEM((1, w), f32),
            pltpu.VMEM((nx * ny, 1, w), f32),
            pltpu.VMEM((1, w), f32),
            pltpu.SMEM((w,), jnp.int32),
            plane, plane,
            pltpu.VMEM((2 * nk * (h + 8), w), f32),
            dma((10,)), dma((4,)), dma((4,)), dma((2,)), dma((2,)),
            dma((nx - 1,)), dma((nx - 1,)), dma, dma, dma, dma,
        ],
        compiler_params=pltpu.CompilerParams(
            collective_id=0, has_side_effects=True, vmem_limit_bytes=vmem
        ),
        name="tracer_step",
    )(
        t.reshape(nk * h, w), s.reshape(nk * h, w), uv.reshape(2 * nk * h, w),
        sea, layers, area, rain, seam,
    )
    t_next, s_next = pl.pallas_call(
        functools.partial(store_kernel, nk, h, w),
        out_shape=[jax.ShapeDtypeStruct((nk * h, w), f32)] * 2,
        in_specs=[pl.BlockSpec(memory_space=pltpu.VMEM)] * 3,
        out_specs=[any_space] * 2,
        scratch_shapes=[pltpu.VMEM((nk * h, w), f32)] * 2 + [dma((2 * store_cuts,))],
        compiler_params=pltpu.CompilerParams(vmem_limit_bytes=8 << 20),
        name="store",
    )(t_next, s_next, side)
    return t_next.reshape(t.shape), s_next.reshape(s.shape)


def solution(mesh):
    in_specs = (
        P("groups", "gy", "gx"),
        P("groups", "gy", "gx"),
        P("groups", None, "gy", "gx"),
        P("gy", "gx"),
        P("gy", "gx"),
        P("gy", "gx"),
        P("gy", "gx"),
        P("gx"),
    )
    out_specs = (P("groups", "gy", "gx"), P("groups", "gy", "gx"))
    return jax.shard_map(
        functools.partial(shards, mesh.shape["gx"], mesh.shape["gy"]),
        mesh=mesh, in_specs=in_specs, out_specs=out_specs, check_vma=False,
    )
```

time: 11.5 us -> 11.2 us (0.974)
  Pallas kernels: 10.7 us -> 10.4 us
    pallas_call x1, Pallas kernels: 9.56 us -> 9.15 us  [shards(): pl.pallas_call(functools.partial(kernel, nx, ny, nk, h, w), out_shape=[pl...]
where the time goes in v2:
time: 11.2 us; the launch traced here: 11 us
  Pallas kernels  10.4 us (93%)
  between operations  0.64 us (6%)
    pallas_call x1, Pallas kernels, shards(): pl.pallas_call(functools.partial(kernel, nx, ny, nk, h, w), out_shape=[pl...  9.15 us
    pallas_call x1, Pallas kernels, shards(): pl.pallas_call(functools.partial(store_kernel, nk, h, w), out_shape=[jax....  1.23 us

profile of v2, /device:TPU:0, one launch (start us, length us, event | category | flops | bytes accessed | tf_op | source)
XLA Modules:
  0.0 11.0 jit_solution(4066117523637246859)
XLA Ops:
  0.6 9.2 %tracer_step.1 = (f32[1024,128]{1,0:T(8,128)S(1)}, f32[1024,128]{1,0:T(8,128)S(1)}, f32[392,128]{1,0:T(8,128)S(1)}) custom-call(f32[1024,128]{1,0:T(8,128)} %bitcast.6, f32[1024,128]{1,0:T(8,128)} %bitcast.7, f32[2048,128]{1,0:T(8,128)} %bitcast.5, s32[64,128]{1,0:T(8,128)} %sea_hbm.1, s32[64,128]{1,0:T(8,128)} %lay_hbm.1, f32[64,128]{1,0:T(8,128)} %area_hbm.1, ...), custom_call_target="tpu_custom_call" | custom-call | tf_op jit(solution)/shard_map/tracer_step/pallas_call | solution.py:516
  9.8 1.2 %store.1 = (f32[1024,128]{1,0:T(8,128)}, f32[1024,128]{1,0:T(8,128)}) custom-call(f32[1024,128]{1,0:T(8,128)S(1)} %get-tuple-element.7.t_ref, f32[1024,128]{1,0:T(8,128)S(1)} %get-tuple-element.8.s_ref, f32[392,128]{1,0:T(8,128)S(1)} %get-tuple-element.9.side_ref), custom_call_target="tpu_custom_call" | custom-call | tf_op jit(solution)/shard_map/store/pallas_call | solution.py:551

commit v3 on v2

--- a/solution.py
+++ b/solution.py
@@ -13,7 +13,7 @@
 top_thickness = 0.5
 
 block_rows = 16
-hubs = 2
+hub_column = 1
 
 MESH = pl.DeviceIdType.MESH
 
@@ -40,7 +40,7 @@
     pack_v, last_v, first_v, east_v, west_v, up_v, down_v, south_v, north_v, fold_v,
     part_v, parts_v, total_v, seam_smem, depth_east_v, depth_north_v, flux_v,
     load_sems, pack_send, pack_recv, row_send, row_recv, fold_send, fold_recv,
-    part_send, part_recv, total_send, total_recv,
+    part_send, part_recv, total_send, total_recv, ready,
 ):
     mx, my = lax.axis_index("gx"), lax.axis_index("gy")
     is_top = my == ny - 1
@@ -49,17 +49,31 @@
     barrier = pltpu.get_barrier_semaphore()
 
     east, west = lax.rem(mx + 1, nx), lax.rem(mx + nx - 1, nx)
-    is_hub = mx < hubs
-    outside = jnp.logical_not(is_hub)
+    near = ny // 2
+    hubs = near + ny
+
+    def hub(gx, gy):
+        return (gx == hub_column) | ((gx == 0) & (gy < near))
+
+    is_hub = hub(mx, my)
+    plain = jnp.logical_not(is_hub)
+    seam_west = mx == 0
+    seam_east = mx == nx - 1
+    has_north, has_south = my < ny - 1, my > 0
 
     def count(flag):
         return jnp.where(flag, 1, 0)
 
-    far_sides = count(east >= hubs) + count(west >= hubs)
+    row_partners = jnp.where(
+        is_top,
+        nx - 1 - count(mx != hub_column),
+        count(jnp.logical_not(hub(east, my)))
+        + count(jnp.logical_not(hub(west, my) | seam_west)),
+    )
     partners = (
-        hubs * ny - count(is_hub) + far_sides
-        + jnp.where(outside, count(my > 0) + count(my < ny - 1), 0)
-        + jnp.where(is_top, nx - hubs - count(outside) - far_sides, 0)
+        hubs - count(is_hub) + row_partners
+        + count(has_north & jnp.logical_not(hub(mx, my + 1)))
+        + count(has_south & jnp.logical_not(hub(mx, my - 1)))
     )
 
     def signal(gx, gy):
@@ -76,16 +90,19 @@
 
             repeat(peers, one)
 
-        @pl.when(outside)
+        @pl.when(plain & is_top)
+        def _():
+            repeat(nx - 1, lambda d: signal(lax.rem(mx + 1 + d, nx), my))
+
+        @pl.when(plain & has_north)
         def _():
             signal(west, my)
-            signal(east, my)
-            pl.when(my > 0)(lambda: signal(mx, my - 1))
-            pl.when(my < ny - 1)(lambda: signal(mx, my + 1))
-
-        @pl.when(outside & is_top)
+            pl.when(jnp.logical_not(seam_east))(lambda: signal(east, my))
+            signal(mx, my + 1)
+
+        @pl.when(plain & has_south)
         def _():
-            repeat(nx - 3, lambda d: signal(lax.rem(mx + 2 + d, nx), my))
+            signal(mx, my - 1)
 
     loads = [
         pltpu.make_async_copy(src, dst, load_sems.at[i])
@@ -136,12 +153,12 @@
     me = mx * ny + my
     parts_v[me] = part
 
-    def send_part(r):
-        @pl.when(r != me)
+    def send_part(gx, gy):
+        @pl.when(gx * ny + gy != me)
         def _():
             pltpu.make_async_remote_copy(
                 src_ref=part_v, dst_ref=parts_v.at[me], send_sem=part_send, recv_sem=part_recv,
-                device_id={"gx": r // ny, "gy": r % ny}, device_id_type=MESH,
+                device_id={"gx": gx, "gy": gy}, device_id_type=MESH,
             ).start()
 
     def several(ref, n, sends, arrivals):
@@ -151,18 +168,23 @@
             device_id={"gx": east}, device_id_type=MESH,
         )
 
-    def hand_on(d):
+    def hand_on(gx, gy):
         return pltpu.make_async_remote_copy(
             src_ref=total_v, dst_ref=total_v, send_sem=total_send, recv_sem=total_recv,
-            device_id={"gx": hubs + d}, device_id_type=MESH,
+            device_id={"gx": gx, "gy": gy}, device_id_type=MESH,
         )
 
     def meet():
         pl.semaphore_wait(barrier, partners)
-        repeat(hubs * ny, send_part)
-
-    early = mx == 0
-    pl.when(jnp.logical_not(early))(meet)
+        repeat(near, lambda gy: send_part(0, gy))
+        repeat(ny, lambda gy: send_part(hub_column, gy))
+        pl.when(seam_east)(
+            lambda: pl.semaphore_signal(ready, inc=1, device_id={"gx": east}, device_id_type=MESH)
+        )
+
+    early = seam_west & (my < near)
+    pack_first = (mx > 0) & (my < near)
+    pl.when(my >= near)(meet)
 
     loads[4].wait()
     depth = (sea * lay_v[...]).astype(jnp.float32)
@@ -225,7 +247,12 @@
 
     for b in (0, 1):
         finish(b)
-        pl.when(jnp.logical_not(early))(to_east[b].start)
+    pl.when(pack_first)(meet)
+
+    @pl.when(jnp.logical_not(early))
+    def _():
+        for b in (0, 1):
+            to_east[b].start()
 
     depth_east_v[...] = jnp.where(
         lane == w - 1, 0.0, jnp.minimum(depth, pltpu.roll(depth, w - 1, 1))
@@ -277,8 +304,11 @@
         for b in (0, 1):
             to_east[b].start()
 
-    for b in (0, 1):
-        to_west[b].start()
+    @pl.when(jnp.logical_not(seam_west))
+    def _():
+        for b in (0, 1):
+            to_west[b].start()
+
     @pl.when(jnp.logical_not(early))
     def _():
         for load in loads[8:]:
@@ -346,6 +376,12 @@
             at = pl.ds(h - 1, nk, stride=h)
             out[at, :] -= g_v[h - 1 : h, :] * (near_weight * near + far_weight * far)
 
+    @pl.when(seam_west)
+    def _():
+        pl.semaphore_wait(ready, 1)
+        for b in (0, 1):
+            to_west[b].start()
+
     @pl.when(jnp.logical_not(is_top))
     def _():
         to_north.wait_send()
@@ -377,9 +413,16 @@
         several(parts_v, peers, part_send, part_recv).wait_recv()
         total_v[...] = jnp.sum(parts_v[...], axis=0)
 
-    @pl.when(mx == hubs - 1)
-    def _():
-        repeat(nx - hubs, lambda d: hand_on(d).start())
+    in_column = mx == hub_column
+    seam_giver = seam_west & (my == near - 1)
+
+    @pl.when(in_column)
+    def _():
+        repeat(nx - 2, lambda d: hand_on(hub_column + 1 + d, my).start())
+
+    @pl.when(seam_giver)
+    def _():
+        repeat(ny - near, lambda d: hand_on(0, near + d).start())
 
     @pl.when(is_top)
     def _():
@@ -417,16 +460,20 @@
 
     @pl.when(is_hub)
     def _():
-        several(parts_v, hubs * ny - 1, part_send, part_recv).wait_send()
-
-    @pl.when(outside)
-    def _():
-        several(parts_v, hubs * ny, part_send, part_recv).wait_send()
-        hand_on(0).wait_recv()
-
-    @pl.when(mx == hubs - 1)
-    def _():
-        several(parts_v, nx - hubs, total_send, total_recv).wait_send()
+        several(parts_v, hubs - 1, part_send, part_recv).wait_send()
+
+    @pl.when(plain)
+    def _():
+        several(parts_v, hubs, part_send, part_recv).wait_send()
+        hand_on(0, 0).wait_recv()
+
+    @pl.when(in_column)
+    def _():
+        several(parts_v, nx - 2, total_send, total_recv).wait_send()
+
+    @pl.when(seam_giver)
+    def _():
+        several(parts_v, ny - near, total_send, total_recv).wait_send()
 
     side_out[pl.ds(6 * h, 8), :] = jnp.broadcast_to(total_v[...], (8, w))
     for b in (0, 1):
@@ -505,7 +552,7 @@
 
 def shards(nx, ny, t, s, uv, sea, layers, area, rain, seam):
     nk, h, w = t.shape
-    assert w == 128 and h % 16 == 0 and nk & (nk - 1) == 0 and nk % 8 == 0 and 6 * nk + 3 <= w and nx > 3 and hubs == 2
+    assert w == 128 and h % 16 == 0 and nk & (nk - 1) == 0 and nk % 8 == 0 and 6 * nk + 3 <= w and nx > 3
     f32 = jnp.float32
     peers = nx * ny - 1
     half_plane = pltpu.VMEM((h // 2, w), f32)
@@ -538,7 +585,7 @@
             plane, plane,
             pltpu.VMEM((2 * nk * (h + 8), w), f32),
             dma((10,)), dma((4,)), dma((4,)), dma((2,)), dma((2,)),
-            dma((nx - 1,)), dma((nx - 1,)), dma, dma, dma, dma,
+            dma((nx - 1,)), dma((nx - 1,)), dma, dma, dma, dma, pltpu.SemaphoreType.REGULAR,
         ],
         compiler_params=pltpu.CompilerParams(
             collective_id=0, has_side_effects=True, vmem_limit_bytes=vmem

time: 11.2 us -> 11.1 us (level)
  no operation moved by 1% of the time
where the time goes in v3:
time: 11.1 us; the launch traced here: 10.9 us
  Pallas kernels  10.3 us (93%)
  between operations  0.64 us (6%)
    pallas_call x1, Pallas kernels, shards(): pl.pallas_call(functools.partial(kernel, nx, ny, nk, h, w), out_shape=[pl...  9.07 us
    pallas_call x1, Pallas kernels, shards(): pl.pallas_call(functools.partial(store_kernel, nk, h, w), out_shape=[jax....  1.23 us

profile of v3, /device:TPU:0, one launch (start us, length us, event | category | flops | bytes accessed | tf_op | source)
XLA Modules:
  0.0 10.9 jit_solution(8104223143899665763)
XLA Ops:
  0.6 9.1 %tracer_step.1 = (f32[1024,128]{1,0:T(8,128)S(1)}, f32[1024,128]{1,0:T(8,128)S(1)}, f32[392,128]{1,0:T(8,128)S(1)}) custom-call(f32[1024,128]{1,0:T(8,128)} %bitcast.6, f32[1024,128]{1,0:T(8,128)} %bitcast.7, f32[2048,128]{1,0:T(8,128)} %bitcast.5, s32[64,128]{1,0:T(8,128)} %sea_hbm.1, s32[64,128]{1,0:T(8,128)} %lay_hbm.1, f32[64,128]{1,0:T(8,128)} %area_hbm.1, ...), custom_call_target="tpu_custom_call" | custom-call | tf_op jit(solution)/shard_map/tracer_step/pallas_call | solution.py:563
  9.7 1.2 %store.1 = (f32[1024,128]{1,0:T(8,128)}, f32[1024,128]{1,0:T(8,128)}) custom-call(f32[1024,128]{1,0:T(8,128)S(1)} %get-tuple-element.7.t_ref, f32[1024,128]{1,0:T(8,128)S(1)} %get-tuple-element.8.s_ref, f32[392,128]{1,0:T(8,128)S(1)} %get-tuple-element.9.side_ref), custom_call_target="tpu_custom_call" | custom-call | tf_op jit(solution)/shard_map/store/pallas_call | solution.py:598

commit v4 on v3

--- a/solution.py
+++ b/solution.py
@@ -50,10 +50,10 @@
 
     east, west = lax.rem(mx + 1, nx), lax.rem(mx + nx - 1, nx)
     near = ny // 2
-    hubs = near + ny
+    hubs = near + 1 + ny
 
     def hub(gx, gy):
-        return (gx == hub_column) | ((gx == 0) & (gy < near))
+        return (gx == hub_column) | ((gx == 0) & ((gy < near) | (gy == ny - 1)))
 
     is_hub = hub(mx, my)
     plain = jnp.logical_not(is_hub)
@@ -66,7 +66,7 @@
 
     row_partners = jnp.where(
         is_top,
-        nx - 1 - count(mx != hub_column),
+        nx - 2 - count(mx > hub_column),
         count(jnp.logical_not(hub(east, my)))
         + count(jnp.logical_not(hub(west, my) | seam_west)),
     )
@@ -105,7 +105,7 @@
             signal(mx, my - 1)
 
     loads = [
-        pltpu.make_async_copy(src, dst, load_sems.at[i])
+        pltpu.make_async_copy(src, dst, load_sems.at[max(i - 4, 0)])
         for i, (src, dst) in enumerate(
             [
                 (area_hbm, area_v),
@@ -132,8 +132,8 @@
     for i in range(2 * nk):
         flux_v[pl.ds(i * (h + 8), 8), :] = zeros
 
-    for load in loads[:4]:
-        load.wait()
+    small = pl.ds(0, 5 * h)
+    pltpu.make_async_copy(t_hbm.at[small], t_v.at[small], load_sems.at[0]).wait()
     area = area_v[...]
     sea = sea_v[...]
     wet_area = area * sea.astype(jnp.float32)
@@ -177,6 +177,7 @@
     def meet():
         pl.semaphore_wait(barrier, partners)
         repeat(near, lambda gy: send_part(0, gy))
+        send_part(0, ny - 1)
         repeat(ny, lambda gy: send_part(hub_column, gy))
         pl.when(seam_east)(
             lambda: pl.semaphore_signal(ready, inc=1, device_id={"gx": east}, device_id_type=MESH)
@@ -186,7 +187,6 @@
     pack_first = (mx > 0) & (my < near)
     pl.when(my >= near)(meet)
 
-    loads[4].wait()
     depth = (sea * lay_v[...]).astype(jnp.float32)
     depth_v[...] = depth
 
@@ -234,16 +234,16 @@
         last_v[at, :] = jnp.where(even_half[:quarter], upper, lower)
         first_v[at, :] = jnp.where(even_half[:quarter], lower, upper)
 
-    def strip(b, src, dst, n, step):
+    def strip(b, src, dst, step):
         at = pl.ds(b * quarter, quarter)
         return pltpu.make_async_remote_copy(
             src_ref=src.at[at], dst_ref=dst.at[at],
-            send_sem=pack_send.at[2 * b + n], recv_sem=pack_recv.at[2 * b + n],
+            send_sem=pack_send, recv_sem=pack_recv,
             device_id={"gx": lax.rem(mx + step, nx)}, device_id_type=MESH,
         )
 
-    to_east = [strip(b, last_v, west_v, 0, 1) for b in (0, 1)]
-    to_west = [strip(b, first_v, east_v, 1, nx - 1) for b in (0, 1)]
+    to_east = [strip(b, last_v, west_v, 1) for b in (0, 1)]
+    to_west = [strip(b, first_v, east_v, nx - 1) for b in (0, 1)]
 
     for b in (0, 1):
         finish(b)
@@ -344,7 +344,7 @@
     def fold_copy(d):
         return pltpu.make_async_remote_copy(
             src_ref=fold_v.at[mx], dst_ref=fold_v.at[mx],
-            send_sem=fold_send.at[d], recv_sem=fold_recv.at[d],
+            send_sem=fold_send, recv_sem=fold_recv,
             device_id={"gx": lax.rem(mx + d + 1, nx)}, device_id_type=MESH,
         )
 
@@ -407,33 +407,6 @@
                 near_weight * south_v[pl.ds(i * nk, nk), :]
                 + far_weight * down_v[pl.ds(i * nk, nk), :]
             )
-
-    @pl.when(is_hub)
-    def _():
-        several(parts_v, peers, part_send, part_recv).wait_recv()
-        total_v[...] = jnp.sum(parts_v[...], axis=0)
-
-    in_column = mx == hub_column
-    seam_giver = seam_west & (my == near - 1)
-
-    @pl.when(in_column)
-    def _():
-        repeat(nx - 2, lambda d: hand_on(hub_column + 1 + d, my).start())
-
-    @pl.when(seam_giver)
-    def _():
-        repeat(ny - near, lambda d: hand_on(0, near + d).start())
-
-    @pl.when(is_top)
-    def _():
-        repeat(nx - 1, lambda d: fold_copy(d).wait())
-        partner = fold_v[seam_smem[0] // w]
-        north_edge(
-            partner[:nk],
-            partner[nk : 2 * nk],
-            0.5 * (up_v[pl.ds(2 * nk, nk), :] - partner[2 * nk : 3 * nk]),
-            partner[3 * nk : 3 * nk + 1],
-        )
 
     def column(plane, at):
         return jnp.broadcast_to(plane[:, at : at + 1], (h, w))
@@ -460,6 +433,33 @@
 
     @pl.when(is_hub)
     def _():
+        several(parts_v, peers, part_send, part_recv).wait_recv()
+        total_v[...] = jnp.sum(parts_v[...], axis=0)
+
+    in_column = mx == hub_column
+    seam_giver = seam_west & is_top
+
+    @pl.when(in_column)
+    def _():
+        repeat(nx - 2, lambda d: hand_on(hub_column + 1 + d, my).start())
+
+    @pl.when(seam_giver)
+    def _():
+        repeat(ny - 1 - near, lambda d: hand_on(0, near + d).start())
+
+    @pl.when(is_top)
+    def _():
+        several(fold_v, nx - 1, fold_send, fold_recv).wait()
+        partner = fold_v[seam_smem[0] // w]
+        north_edge(
+            partner[:nk],
+            partner[nk : 2 * nk],
+            0.5 * (up_v[pl.ds(2 * nk, nk), :] - partner[2 * nk : 3 * nk]),
+            partner[3 * nk : 3 * nk + 1],
+        )
+
+    @pl.when(is_hub)
+    def _():
         several(parts_v, hubs - 1, part_send, part_recv).wait_send()
 
     @pl.when(plain)
@@ -473,12 +473,10 @@
 
     @pl.when(seam_giver)
     def _():
-        several(parts_v, ny - near, total_send, total_recv).wait_send()
+        several(parts_v, ny - 1 - near, total_send, total_recv).wait_send()
 
     side_out[pl.ds(6 * h, 8), :] = jnp.broadcast_to(total_v[...], (8, w))
-    for b in (0, 1):
-        to_east[b].wait()
-        to_west[b].wait()
+    several(pack_v, h, pack_send, pack_recv).wait()
     side_out[pl.ds(5 * h, half), :] = west_v[...]
     side_out[pl.ds(5 * h + half, half), :] = east_v[...]
 
@@ -486,7 +484,7 @@
 store_cuts = 4
 
 
-def store_kernel(nk, h, w, t_ref, s_ref, side_ref, t_hbm, s_hbm, t_v, s_v, sems):
+def store_kernel(nk, h, w, t_ref, s_ref, side_ref, t_hbm, s_hbm, t_v, s_v, sem):
     half = h // 2
     mine, own_speed, edge_gain, surface, surface_wet = (
         side_ref[pl.ds(i * h, h), :] for i in range(5)
@@ -530,7 +528,6 @@
 
     at_edge = (lane[:half] == 0) | (lane[:half] == w - 1)
     step = nk // store_cuts
-    copies = []
     for i, (ref, out, hbm) in enumerate(((t_ref, t_v, t_hbm), (s_ref, s_v, s_hbm))):
         for cut in reversed(range(store_cuts)):
             for k in range(cut * step, (cut + 1) * step):
@@ -543,16 +540,14 @@
                     at = pl.ds(k * h + part * half, half)
                     out[at, :] = ref[at, :] + change
             at = pl.ds(cut * step * h, step * h)
-            copy = pltpu.make_async_copy(out.at[at], hbm.at[at], sems.at[len(copies)])
-            copy.start()
-            copies.append(copy)
-    for copy in copies:
-        copy.wait()
+            pltpu.make_async_copy(out.at[at], hbm.at[at], sem).start()
+    for out, hbm in ((t_v, t_hbm), (s_v, s_hbm)):
+        pltpu.make_async_copy(out, hbm, sem).wait()
 
 
 def shards(nx, ny, t, s, uv, sea, layers, area, rain, seam):
     nk, h, w = t.shape
-    assert w == 128 and h % 16 == 0 and nk & (nk - 1) == 0 and nk % 8 == 0 and 6 * nk + 3 <= w and nx > 3
+    assert w == 128 and h % 16 == 0 and nk & (nk - 1) == 0 and nk % 8 == 0 and 6 * nk + 3 <= w and nx > 3 and ny > 3
     f32 = jnp.float32
     peers = nx * ny - 1
     half_plane = pltpu.VMEM((h // 2, w), f32)
@@ -584,8 +579,8 @@
             pltpu.SMEM((w,), jnp.int32),
             plane, plane,
             pltpu.VMEM((2 * nk * (h + 8), w), f32),
-            dma((10,)), dma((4,)), dma((4,)), dma((2,)), dma((2,)),
-            dma((nx - 1,)), dma((nx - 1,)), dma, dma, dma, dma, pltpu.SemaphoreType.REGULAR,
+            dma((6,)), dma, dma, dma((2,)), dma((2,)),
+            dma, dma, dma, dma, dma, dma, pltpu.SemaphoreType.REGULAR,
         ],
         compiler_params=pltpu.CompilerParams(
             collective_id=0, has_side_effects=True, vmem_limit_bytes=vmem
@@ -600,7 +595,7 @@
         out_shape=[jax.ShapeDtypeStruct((nk * h, w), f32)] * 2,
         in_specs=[pl.BlockSpec(memory_space=pltpu.VMEM)] * 3,
         out_specs=[any_space] * 2,
-        scratch_shapes=[pltpu.VMEM((nk * h, w), f32)] * 2 + [dma((2 * store_cuts,))],
+        scratch_shapes=[pltpu.VMEM((nk * h, w), f32)] * 2 + [dma],
         compiler_params=pltpu.CompilerParams(vmem_limit_bytes=8 << 20),
         name="store",
     )(t_next, s_next, side)

time: 11.1 us -> 10.8 us (0.973)
  Pallas kernels: 10.3 us -> 9.99 us
    pallas_call x1, Pallas kernels: 9.07 us -> 8.82 us  [shards(): pl.pallas_call(functools.partial(kernel, nx, ny, nk, h, w), out_shape=[pl...]
where the time goes in v4:
time: 10.8 us; the launch traced here: 10.6 us
  Pallas kernels  9.99 us (92%)
  between operations  0.64 us (6%)
    pallas_call x1, Pallas kernels, shards(): pl.pallas_call(functools.partial(kernel, nx, ny, nk, h, w), out_shape=[pl...  8.82 us
    pallas_call x1, Pallas kernels, shards(): pl.pallas_call(functools.partial(store_kernel, nk, h, w), out_shape=[jax....  1.17 us

profile of v4, /device:TPU:0, one launch (start us, length us, event | category | flops | bytes accessed | tf_op | source)
XLA Modules:
  0.0 10.6 jit_solution(6933701800272644805)
XLA Ops:
  0.6 8.8 %tracer_step.1 = (f32[1024,128]{1,0:T(8,128)S(1)}, f32[1024,128]{1,0:T(8,128)S(1)}, f32[392,128]{1,0:T(8,128)S(1)}) custom-call(f32[1024,128]{1,0:T(8,128)} %bitcast.6, f32[1024,128]{1,0:T(8,128)} %bitcast.7, f32[2048,128]{1,0:T(8,128)} %bitcast.5, s32[64,128]{1,0:T(8,128)} %sea_hbm.1, s32[64,128]{1,0:T(8,128)} %lay_hbm.1, f32[64,128]{1,0:T(8,128)} %area_hbm.1, ...), custom_call_target="tpu_custom_call" | custom-call | tf_op jit(solution)/shard_map/tracer_step/pallas_call | solution.py:558
  9.5 1.2 %store.1 = (f32[1024,128]{1,0:T(8,128)}, f32[1024,128]{1,0:T(8,128)}) custom-call(f32[1024,128]{1,0:T(8,128)S(1)} %get-tuple-element.7.t_ref, f32[1024,128]{1,0:T(8,128)S(1)} %get-tuple-element.8.s_ref, f32[392,128]{1,0:T(8,128)S(1)} %get-tuple-element.9.side_ref), custom_call_target="tpu_custom_call" | custom-call | tf_op jit(solution)/shard_map/store/pallas_call | solution.py:593

commit v5 on v4

--- a/solution.py
+++ b/solution.py
@@ -481,7 +481,7 @@
     side_out[pl.ds(5 * h + half, half), :] = east_v[...]
 
 
-store_cuts = 4
+store_cuts = 16
 
 
 def store_kernel(nk, h, w, t_ref, s_ref, side_ref, t_hbm, s_hbm, t_v, s_v, sem):

time: 10.8 us -> 10.7 us (level)
  no operation moved by 1% of the time
where the time goes in v5:
time: 10.7 us; the launch traced here: 10.6 us
  Pallas kernels  9.95 us (93%)
  between operations  0.64 us (6%)
    pallas_call x1, Pallas kernels, shards(): pl.pallas_call(functools.partial(kernel, nx, ny, nk, h, w), out_shape=[pl...  8.82 us
    pallas_call x1, Pallas kernels, shards(): pl.pallas_call(functools.partial(store_kernel, nk, h, w), out_shape=[jax....  1.13 us

profile of v5, /device:TPU:0, one launch (start us, length us, event | category | flops | bytes accessed | tf_op | source)
XLA Modules:
  0.0 10.6 jit_solution(17060657660951707943)
XLA Ops:
  0.6 8.8 %tracer_step.1 = (f32[1024,128]{1,0:T(8,128)S(1)}, f32[1024,128]{1,0:T(8,128)S(1)}, f32[392,128]{1,0:T(8,128)S(1)}) custom-call(f32[1024,128]{1,0:T(8,128)} %bitcast.6, f32[1024,128]{1,0:T(8,128)} %bitcast.7, f32[2048,128]{1,0:T(8,128)} %bitcast.5, s32[64,128]{1,0:T(8,128)} %sea_hbm.1, s32[64,128]{1,0:T(8,128)} %lay_hbm.1, f32[64,128]{1,0:T(8,128)} %area_hbm.1, ...), custom_call_target="tpu_custom_call" | custom-call | tf_op jit(solution)/shard_map/tracer_step/pallas_call | solution.py:558
  9.5 1.1 %store.1 = (f32[1024,128]{1,0:T(8,128)}, f32[1024,128]{1,0:T(8,128)}) custom-call(f32[1024,128]{1,0:T(8,128)S(1)} %get-tuple-element.7.t_ref, f32[1024,128]{1,0:T(8,128)S(1)} %get-tuple-element.8.s_ref, f32[392,128]{1,0:T(8,128)S(1)} %get-tuple-element.9.side_ref), custom_call_target="tpu_custom_call" | custom-call | tf_op jit(solution)/shard_map/store/pallas_call | solution.py:593
